TPU v7x, 32 devices: a whole 2x2x4 slice. The times are simulated.
32 devices in a mesh: ty: 4 (over y, x), tx: 8 (over z, core).
Axes of the slice: x: 2, y: 2, z: 4, core: 2. Of those that a mesh axis runs over, the one named last changes fastest.
Arguments:
- object_slices: float32 [2, 2, 1024, 2048], P(None, None, 'ty', 'tx'), may hold values from -5 to 5
- probe: float32 [2, 256, 256], replicated, may hold values from -5 to 5
- position_count: int32 [4, 8], P('ty', 'tx'), may hold values from 1 to 5, as said below
- offsets: int32 [4, 8, 5, 2], P('ty', 'tx'), may hold values from 0 to 128
- intensities: float32 [4, 8, 5, 256, 256], P('ty', 'tx'), may hold values from 0 to 2
Outputs:
- object_new: float32 [2, 2, 1024, 2048], P(None, None, 'ty', 'tx')
- probe_new: float32 [2, 256, 256], replicated
Inputs may be any that keep to these rules, and one draw needn't show every extreme that they name: `position_count`: each tile has 1 to 5 positions; some tile has exactly 5.
All inputs are finite; a program needn't handle non-finite values.
Results may differ from a plain program's by a relative error of at most 0.0003.
Values sent between devices are 32-bit elements; how exact they have to be, the bound alone decides.
No kernel may reach another device: no remote copies, remote signals or barrier semaphores. Data moves between devices by JAX's collectives and lax.ppermute only.
A program may use at most 128 MiB of HBM per device.

v0:
```python
import math
import jax
import jax.numpy as jnp
from jax import lax
from jax.sharding import PartitionSpec as P

PROBE = 256
CORE = 256
MARGIN = 64
ITERS = 2
chirp_rate = 0.5
object_rate = 0.5
probe_rate = 2.0


def extended_2(block, sides, width):
    for axis, dim in sides:
        count = lax.axis_size(axis)
        forward = [(i, i + 1) for i in range(count - 1)]
        forward.append((count - 1, 0))
        backward = [(target, source) for source, target in forward]
        low = lax.ppermute(
            lax.slice_in_dim(block, block.shape[dim] - width, None, axis=dim), axis, forward
        )
        high = lax.ppermute(lax.slice_in_dim(block, 0, width, axis=dim), axis, backward)
        block = jnp.concatenate([low, block, high], axis=dim)
    return block


def matmul(left, right):
    return jnp.dot(left, right, precision=lax.Precision.HIGHEST, preferred_element_type=jnp.float32)


def complex_product(left_real, left_imag, right_real, right_imag):
    out_real = matmul(left_real, right_real) - matmul(left_imag, right_imag)
    out_imag = matmul(left_real, right_imag) + matmul(left_imag, right_real)
    return (out_real, out_imag)


def dft_tables(size):
    index = lax.iota(jnp.int32, size)
    product = index[:, None] * index[None, :] % size
    angles = product.astype(jnp.float32) * (2.0 * math.pi / size)
    factor = 1.0 / math.sqrt(size)
    four_real = jnp.cos(angles) * factor
    four_imag = -jnp.sin(angles) * factor
    centred = ((index + size // 2) % size - size // 2).astype(jnp.float32)
    phases = centred * centred * (chirp_rate * math.pi / size)
    kernel_real = jnp.cos(phases)
    kernel_imag = -jnp.sin(phases)
    scaled_real = four_real * kernel_real[None, :] + four_imag * kernel_imag[None, :]
    scaled_imag = four_real * kernel_imag[None, :] - four_imag * kernel_real[None, :]
    prop_real, prop_imag = complex_product(scaled_real, scaled_imag, four_real, four_imag)
    return (four_real, four_imag, prop_real, prop_imag)


def forward_pair(mat_real, mat_imag, field_real, field_imag):
    mid_real, mid_imag = complex_product(mat_real, mat_imag, field_real, field_imag)
    return complex_product(mid_real, mid_imag, mat_real.T, mat_imag.T)


def adjoint_pair(mat_real, mat_imag, field_real, field_imag):
    mid_real, mid_imag = complex_product(mat_real.T, -mat_imag.T, field_real, field_imag)
    return complex_product(mid_real, mid_imag, mat_real, -mat_imag)


def position_grad(probe_now, window, measured, tables):
    four_real, four_imag, prop_real, prop_imag = tables
    probe_real, probe_imag = (probe_now[0], probe_now[1])
    one_real, one_imag, two_real, two_imag = (window[0], window[1], window[2], window[3])
    wave_real = probe_real * one_real - probe_imag * one_imag
    wave_imag = probe_real * one_imag + probe_imag * one_real
    moved_real, moved_imag = forward_pair(prop_real, prop_imag, wave_real, wave_imag)
    exit_real = moved_real * two_real - moved_imag * two_imag
    exit_imag = moved_real * two_imag + moved_imag * two_real
    far_real, far_imag = forward_pair(four_real, four_imag, exit_real, exit_imag)
    misfit = far_real * far_real + far_imag * far_imag - measured
    back_real, back_imag = adjoint_pair(four_real, four_imag, misfit * far_real, misfit * far_imag)
    grad_two_real = moved_real * back_real + moved_imag * back_imag
    grad_two_imag = moved_real * back_imag - moved_imag * back_real
    gmove_real = two_real * back_real + two_imag * back_imag
    gmove_imag = two_real * back_imag - two_imag * back_real
    gwave_real, gwave_imag = adjoint_pair(prop_real, prop_imag, gmove_real, gmove_imag)
    grad_one_real = probe_real * gwave_real + probe_imag * gwave_imag
    grad_one_imag = probe_real * gwave_imag - probe_imag * gwave_real
    gprobe_real = one_real * gwave_real + one_imag * gwave_imag
    gprobe_imag = one_real * gwave_imag - one_imag * gwave_real
    object_part = jnp.stack([grad_one_real, grad_one_imag, grad_two_real, grad_two_imag])
    return (object_part, jnp.stack([gprobe_real, gprobe_imag]))


def fold_axis(padded, width, dim):
    extent = padded.shape[dim] - 2 * width
    middle = lax.slice_in_dim(padded, width, width + extent, axis=dim)
    before = lax.slice_in_dim(padded, 0, width, axis=dim)
    after = lax.slice_in_dim(padded, width + extent, extent + 2 * width, axis=dim)
    spec_before = [(0, 0)] * padded.ndim
    spec_before[dim] = (2 * MARGIN - width, extent - 2 * MARGIN)
    spec_after = [(0, 0)] * padded.ndim
    spec_after[dim] = (CORE, extent - CORE - width)
    return middle + jnp.pad(before, spec_before) + jnp.pad(after, spec_after)


def fold_sums(padded, width):
    return fold_axis(fold_axis(padded, width, 1), width, 2)


def body(object_slices, probe, position_count, offsets, intensities):
    tables = dft_tables(PROBE)
    extent = CORE + 2 * MARGIN
    zero = jnp.int32(0)
    count = position_count[0, 0]
    core = object_slices.reshape(4, CORE, CORE)
    extended = extended_2(core, (("ty", 1), ("tx", 2)), MARGIN)
    probe_now = probe
    devices = lax.axis_size("ty") * lax.axis_size("tx")
    for step in range(ITERS):

        def visit(slot, carry):
            local, local_probe = carry
            top = offsets[0, 0, slot, 0]
            left = offsets[0, 0, slot, 1]
            window = lax.dynamic_slice(extended, (zero, top, left), (4, PROBE, PROBE))
            object_part, probe_part = position_grad(
                probe_now, window, intensities[0, 0, slot], tables
            )
            current = lax.dynamic_slice(local, (zero, top, left), (4, PROBE, PROBE))
            local = lax.dynamic_update_slice(local, current + object_part, (zero, top, left))
            return (local, local_probe + probe_part)

        start = (
            jnp.zeros((4, extent, extent), jnp.float32),
            jnp.zeros((2, PROBE, PROBE), jnp.float32),
        )
        grads, probe_grad = lax.fori_loop(zero, count, visit, start)
        peak = jnp.max(probe_now[0] * probe_now[0] + probe_now[1] * probe_now[1]) + 1e-06
        padded = extended_2(grads, (("ty", 1), ("tx", 2)), MARGIN)
        total = fold_sums(padded, MARGIN)[:, MARGIN : MARGIN + CORE, MARGIN : MARGIN + CORE]
        core = core - object_rate / peak * total
        if step + 1 < ITERS:
            extended = extended_2(core, (("ty", 1), ("tx", 2)), MARGIN)
        summed = lax.psum(probe_grad, ("ty", "tx"))
        probe_now = probe_now - probe_rate / devices * summed
    return (core.reshape(2, 2, CORE, CORE), probe_now)


def solution(mesh):
    placed = (
        P(None, None, "ty", "tx"),
        P(),
        P("ty", "tx"),
        P("ty", "tx", None, None),
        P("ty", "tx", None, None, None),
    )
    return jax.shard_map(
        body,
        mesh=mesh,
        in_specs=placed,
        out_specs=(P(None, None, "ty", "tx"), P()),
        check_vma=False,
    )
```

profile of v0, /device:TPU:0, one launch (start us, length us, event | category | flops | bytes accessed | tf_op | source)
XLA Modules:
  0.0 1035.9 jit_solution(13837448059332774943)
XLA Ops:
  10.0 3.0 collective-permute-start
  17.1 9.8 collective-permute-done
  26.9 10.6 %collective-permute-done.1 = f32[4,64,256]{1,2,0:T(8,128)S(1)} collective-permute-done((f32[4,64,256]{1,2,0:T(8,128)}, f32[4,64,256]{1,2,0:T(8,128)S(1)}, u32[]{:S(2)}, u32[]{:S(2)}) %collective-permute-start.1) | collective-permute-done | bytes 262176 | tf_op jit(solution)/shard_map/ppermute | solution.py:25
  38.0 3.5 collective-permute-start.3
  44.5 4.6 collective-permute-done.2
  49.1 3.1 pad_maximum_fusion.2
  52.2 1.6 broadcast.114.clone
  54.6 203.5 %while.32 = (s32[]{:T(128)}, f32[4,384,384]{2,1,0:T(8,128)}, f32[2,256,256]{2,1,0:T(8,128)}, s32[]{:T(128)}, s32[1,1,5,2]{2,3,1,0:T(2,128)S(1)}, /*index=5*/f32[...) while((s32[]{:T(128)}, f32[4,384,384]{2,1,0:T(8,128)}, ...), condition=%wide.region_2.3_spmd.clone.clone, body=%wide.region_1.2_spmd.clone.clone.sunk | while | flops 6464077824 | bytes 48234916 | solution.py:135
  83.4 2.5 fusion.635
  103.6 2.4 fusion.646
  116.4 1.6 fusion.651
  123.1 2.0 maximum_add_fusion.8
  125.1 11.5 %dynamic_update_slice.16 = f32[4,384,384]{2,1,0:T(8,128)} dynamic-update-slice(f32[4,384,384]{2,1,0:T(8,128)} %get-tuple-element.1014, f32[4,256,256]{2,1,0:T(8,128)S(1)} %maximum_add_fusion.8, s32[]{:T(128)} %constant.70.clone.1..sunk, s32[]{:T(128)S(6)} %select_n.366, s32[]{:T(128)S(6)} %select_n.367) | dynamic-update-slice | bytes 2097156 | tf_op jit(solution)/shard_map/while/body/dynamic_update_slice | solution.py:128
  141.4 2.5 fusion.635
  161.7 2.4 fusion.646
  174.4 1.6 fusion.651
  181.1 2.0 maximum_add_fusion.8
  183.1 11.3 %dynamic_update_slice.16 = f32[4,384,384]{2,1,0:T(8,128)} dynamic-update-slice(f32[4,384,384]{2,1,0:T(8,128)} %get-tuple-element.1014, f32[4,256,256]{2,1,0:T(8,128)S(1)} %maximum_add_fusion.8, s32[]{:T(128)} %constant.70.clone.1..sunk, s32[]{:T(128)S(6)} %select_n.366, s32[]{:T(128)S(6)} %select_n.367) | dynamic-update-slice | bytes 2097156 | tf_op jit(solution)/shard_map/while/body/dynamic_update_slice | solution.py:128
  199.2 2.5 fusion.635
  219.5 2.4 fusion.646
  232.3 1.6 fusion.651
  238.9 2.0 maximum_add_fusion.8
  240.9 11.5 %dynamic_update_slice.16 = f32[4,384,384]{2,1,0:T(8,128)} dynamic-update-slice(f32[4,384,384]{2,1,0:T(8,128)} %get-tuple-element.1014, f32[4,256,256]{2,1,0:T(8,128)S(1)} %maximum_add_fusion.8, s32[]{:T(128)} %constant.70.clone.1..sunk, s32[]{:T(128)S(6)} %select_n.366, s32[]{:T(128)S(6)} %select_n.367) | dynamic-update-slice | bytes 2097156 | tf_op jit(solution)/shard_map/while/body/dynamic_update_slice | solution.py:128
  259.3 117.1 %collective-permute-start.5 = (f32[4,64,384]{2,1,0:T(8,128)S(1)}, f32[4,64,384]{2,1,0:T(8,128)S(1)}, u32[]{:S(2)}, u32[]{:S(2)}) collective-permute-start(f32[4,64,384]{2,1,0:T(8,128)S(1)} %get-tuple-element.749), channel_id=1, source_target_pairs={{8,0},{16,8},{24,16},{0,24},{9,1},{17,9},{25,17},{1,25},{10,2},{18... | collective-permute-start | bytes 1179656 | tf_op jit(solution)/shard_map/ppermute | solution.py:25
  376.4 3.1 copy.25
  379.5 4.3 collective-permute-done.4
  386.2 2.5 pad_maximum_fusion.9
  388.7 4.3 collective-permute-start.6
  394.3 7.8 collective-permute-done.6
  402.2 2.7 collective-permute-done.7
  404.9 3.0 pad_maximum_fusion
  408.0 2.8 fusion.242
  413.8 8.9 collective-permute-start.8
  422.7 13.3 %collective-permute-done.8 = f32[4,64,256]{1,2,0:T(8,128)S(1)} collective-permute-done((f32[4,64,256]{1,2,0:T(8,128)}, f32[4,64,256]{1,2,0:T(8,128)S(1)}, u32[]{:S(2)}, u32[]{:S(2)}) %collective-permute-start.8) | collective-permute-done | bytes 262176 | tf_op jit(solution)/shard_map/ppermute | solution.py:22
  436.0 11.2 %collective-permute-done.9 = f32[4,64,256]{1,2,0:T(8,128)} collective-permute-done((f32[4,64,256]{1,2,0:T(8,128)}, f32[4,64,256]{1,2,0:T(8,128)}, u32[]{:S(2)}, u32[]{:S(2)}) %collective-permute-start.9) | collective-permute-done | bytes 262176 | tf_op jit(solution)/shard_map/ppermute | solution.py:25
  447.2 2.2 pad_maximum_fusion.12
  449.4 3.5 collective-permute-start.11
  452.9 100.7 %all-reduce.11.cloned.1.call-done = f32[2,256,256]{2,1,0:T(8,128)} async-done(((f32[2,256,256]{2,1,0:T(8,128)}), f32[2,256,256]{2,1,0:T(8,128)}) %all-reduce.11.cloned.1.call-update) | async-done | bytes 524304 | tf_op jit(solution)/shard_map/psum | solution.py:142
  554.7 3.3 pad_maximum_fusion.3
  558.1 1.6 broadcast.114
  560.5 204.1 %while.33 = (s32[]{:T(128)}, f32[4,384,384]{2,1,0:T(8,128)}, f32[2,256,256]{2,1,0:T(8,128)}, s32[]{:T(128)}, s32[1,1,5,2]{2,3,1,0:T(2,128)S(1)}, /*index=5*/f32[...) while((s32[]{:T(128)}, f32[4,384,384]{2,1,0:T(8,128)}, ...), condition=%wide.region_6.7_spmd.clone.clone, body=%wide.region_5.6_spmd.clone.clone.sunk | while | flops 6464077824 | bytes 48234916 | solution.py:135
  589.1 2.5 fusion.709
  609.4 2.4 fusion.720
  629.6 1.8 maximum_add_fusion.10
  631.4 11.5 %dynamic_update_slice.17 = f32[4,384,384]{2,1,0:T(8,128)} dynamic-update-slice(f32[4,384,384]{2,1,0:T(8,128)} %get-tuple-element.1071, f32[4,256,256]{2,1,0:T(8,128)S(1)} %maximum_add_fusion.10, s32[]{:T(128)} %constant.70.clone.1..sunk.1, s32[]{:T(128)S(6)} %select_n.385, s32[]{:T(128)S(6)} %select_n.386) | dynamic-update-slice | bytes 2097156 | tf_op jit(solution)/shard_map/while/body/dynamic_update_slice | solution.py:128
  647.8 2.5 fusion.709
  668.0 2.4 fusion.720
  680.8 1.6 fusion.725
  688.2 1.8 maximum_add_fusion.10
  690.0 11.3 %dynamic_update_slice.17 = f32[4,384,384]{2,1,0:T(8,128)} dynamic-update-slice(f32[4,384,384]{2,1,0:T(8,128)} %get-tuple-element.1071, f32[4,256,256]{2,1,0:T(8,128)S(1)} %maximum_add_fusion.10, s32[]{:T(128)} %constant.70.clone.1..sunk.1, s32[]{:T(128)S(6)} %select_n.385, s32[]{:T(128)S(6)} %select_n.386) | dynamic-update-slice | bytes 2097156 | tf_op jit(solution)/shard_map/while/body/dynamic_update_slice | solution.py:128
  706.2 2.5 fusion.709
  726.4 2.4 fusion.720
  739.2 1.6 fusion.725
  746.7 1.8 maximum_add_fusion.10
  748.5 11.5 %dynamic_update_slice.17 = f32[4,384,384]{2,1,0:T(8,128)} dynamic-update-slice(f32[4,384,384]{2,1,0:T(8,128)} %get-tuple-element.1071, f32[4,256,256]{2,1,0:T(8,128)S(1)} %maximum_add_fusion.10, s32[]{:T(128)} %constant.70.clone.1..sunk.1, s32[]{:T(128)S(6)} %select_n.385, s32[]{:T(128)S(6)} %select_n.386) | dynamic-update-slice | bytes 2097156 | tf_op jit(solution)/shard_map/while/body/dynamic_update_slice | solution.py:128
  765.8 119.2 %collective-permute-start.13 = (f32[4,64,384]{2,1,0:T(8,128)S(1)}, f32[4,64,384]{2,1,0:T(8,128)S(1)}, u32[]{:S(2)}, u32[]{:S(2)}) collective-permute-start(f32[4,64,384]{2,1,0:T(8,128)S(1)} %get-tuple-element.747), channel_id=1, source_target_pairs={{8,0},{16,8},{24,16},{0,24},{9,1},{17,9},{25,17},{1,25},{10,2},{18... | collective-permute-start | bytes 1179656 | tf_op jit(solution)/shard_map/ppermute | solution.py:25
  885.0 3.1 copy.30
  888.1 6.8 collective-permute-done.12
  895.5 2.5 pad_maximum_fusion.6
  898.1 3.4 collective-permute-start.15
  902.9 116.5 %all-reduce.13.cloned.1.call-done = f32[2,256,256]{2,1,0:T(8,128)} async-done(((f32[2,256,256]{2,1,0:T(8,128)}), f32[2,256,256]{2,1,0:T(8,128)}) %all-reduce.13.cloned.1.call-update) | async-done | bytes 524304 | tf_op jit(solution)/shard_map/psum | solution.py:142
  1019.3 1.9 multiply_subtract_fusion
  1021.3 2.9 pad_maximum_fusion.1
  1024.2 1.6 fusion.240
  (315 shorter events, 230.8 us)
Async XLA Ops:
  7.2 546.4 %all-reduce.11.cloned.1.call-start = ((), (), s32[]{:S(2)}) async-start(), calls=%async_computation | async-start | bytes 1048576 | tf_op jit(solution)/shard_map/psum | solution.py:142
  8.8 40.3 %copy-start.3 = (f32[2,2,256,256]{2,3,1,0:T(8,128)}, f32[2,2,256,256]{2,3,1,0:T(8,128)S(1)}, u32[]{:S(2)}) copy-start(f32[2,2,256,256]{2,3,1,0:T(8,128)S(1)} %copy.21) | copy-start | bytes 3145732
  10.0 16.9 %collective-permute-start = (f32[4,64,256]{1,2,0:T(8,128)}, f32[4,64,256]{1,2,0:T(8,128)S(1)}, u32[]{:S(2)}, u32[]{:S(2)}) collective-permute-start(f32[4,64,256]{1,2,0:T(8,128)} %get-tuple-element.756), channel_id=1, source_target_pairs={{0,8},{8,16},{16,24},{24,0},{1,9},{9,17},{17,25},{25,1},{2,10},{10... | collective-permute-start | bytes 786440 | tf_op jit(solution)/shard_map/ppermute | solution.py:22
  13.0 24.6 %collective-permute-start.1 = (f32[4,64,256]{1,2,0:T(8,128)}, f32[4,64,256]{1,2,0:T(8,128)S(1)}, u32[]{:S(2)}, u32[]{:S(2)}) collective-permute-start(f32[4,64,256]{1,2,0:T(8,128)} %get-tuple-element.757), channel_id=1, source_target_pairs={{8,0},{16,8},{24,16},{0,24},{9,1},{17,9},{25,17},{1,25},{10,2},{18... | collective-permute-start | bytes 786440 | tf_op jit(solution)/shard_map/ppermute | solution.py:25
  37.6 5.4 copy-start.12
  37.9 11.2 %collective-permute-start.2 = (f32[4,384,64]{1,2,0:T(8,128)S(1)}, f32[4,384,64]{1,2,0:T(8,128)S(1)}, u32[]{:S(2)}, u32[]{:S(2)}) collective-permute-start(f32[4,384,64]{1,2,0:T(8,128)S(1)} %get-tuple-element.752), channel_id=1, source_target_pairs={{0,1},{1,2},{2,3},{3,4},{4,5},{5,6},{6,7},{7,0},{8,9},{9,10},{10,1... | collective-permute-start | bytes 1179656 | tf_op jit(solution)/shard_map/ppermute | solution.py:22
  38.0 11.1 %collective-permute-start.3 = (f32[4,384,64]{1,2,0:T(8,128)S(1)}, f32[4,384,64]{1,2,0:T(8,128)S(1)}, u32[]{:S(2)}, u32[]{:S(2)}) collective-permute-start(f32[4,384,64]{1,2,0:T(8,128)S(1)} %get-tuple-element.753), channel_id=1, source_target_pairs={{1,0},{2,1},{3,2},{4,3},{5,4},{6,5},{7,6},{0,7},{9,8},{10,9},{11,1... | collective-permute-start | bytes 1179656 | tf_op jit(solution)/shard_map/ppermute | solution.py:25
  44.5 10.1 copy-start
  44.5 10.1 copy-start.13
  119.8 3.1 copy-start.9
  123.1 13.5 %copy-start.10 = (f32[2,256,256]{2,1,0:T(8,128)}, f32[2,256,256]{2,1,0:T(8,128)S(1)}, u32[]{:S(2)}) copy-start(f32[2,256,256]{2,1,0:T(8,128)S(1)} %maximum_add_fusion.9) | copy-start | bytes 1572868 | tf_op jit(solution)/shard_map/while
  177.8 3.1 copy-start.9
  181.1 13.3 %copy-start.10 = (f32[2,256,256]{2,1,0:T(8,128)}, f32[2,256,256]{2,1,0:T(8,128)S(1)}, u32[]{:S(2)}) copy-start(f32[2,256,256]{2,1,0:T(8,128)S(1)} %maximum_add_fusion.9) | copy-start | bytes 1572868 | tf_op jit(solution)/shard_map/while
  235.7 3.1 copy-start.9
  238.9 13.5 %copy-start.10 = (f32[2,256,256]{2,1,0:T(8,128)}, f32[2,256,256]{2,1,0:T(8,128)S(1)}, u32[]{:S(2)}) copy-start(f32[2,256,256]{2,1,0:T(8,128)S(1)} %maximum_add_fusion.9) | copy-start | bytes 1572868 | tf_op jit(solution)/shard_map/while
  259.3 124.5 %collective-permute-start.4 = (f32[4,64,384]{2,1,0:T(8,128)S(1)}, f32[4,64,384]{2,1,0:T(8,128)}, u32[]{:S(2)}, u32[]{:S(2)}) collective-permute-start(f32[4,64,384]{2,1,0:T(8,128)S(1)} %get-tuple-element.748), channel_id=1, source_target_pairs={{0,8},{8,16},{16,24},{24,0},{1,9},{9,17},{17,25},{25,1},{2,10},{10... | collective-permute-start | bytes 1179656 | tf_op jit(solution)/shard_map/ppermute | solution.py:22
  259.3 126.6 %collective-permute-start.5 = (f32[4,64,384]{2,1,0:T(8,128)S(1)}, f32[4,64,384]{2,1,0:T(8,128)S(1)}, u32[]{:S(2)}, u32[]{:S(2)}) collective-permute-start(f32[4,64,384]{2,1,0:T(8,128)S(1)} %get-tuple-element.749), channel_id=1, source_target_pairs={{8,0},{16,8},{24,16},{0,24},{9,1},{17,9},{25,17},{1,25},{10,2},{18... | collective-permute-start | bytes 1179656 | tf_op jit(solution)/shard_map/ppermute | solution.py:25
  388.7 13.5 %collective-permute-start.6 = (f32[4,512,64]{1,2,0:T(8,128)}, f32[4,512,64]{1,2,0:T(8,128)}, u32[]{:S(2)}, u32[]{:S(2)}) collective-permute-start(f32[4,512,64]{1,2,0:T(8,128)} %get-tuple-element.740), channel_id=1, source_target_pairs={{0,1},{1,2},{2,3},{3,4},{4,5},{5,6},{6,7},{7,0},{8,9},{9,10},{10,1... | collective-permute-start | bytes 1572872 | tf_op jit(solution)/shard_map/ppermute | solution.py:22
  393.0 11.9 %collective-permute-start.7 = (f32[4,512,64]{1,2,0:T(8,128)}, f32[4,512,64]{1,2,0:T(8,128)}, u32[]{:S(2)}, u32[]{:S(2)}) collective-permute-start(f32[4,512,64]{1,2,0:T(8,128)} %get-tuple-element.741), channel_id=1, source_target_pairs={{1,0},{2,1},{3,2},{4,3},{5,4},{6,5},{7,6},{0,7},{9,8},{10,9},{11,1... | collective-permute-start | bytes 1572872 | tf_op jit(solution)/shard_map/ppermute | solution.py:25
  394.3 13.6 %copy-start.2 = (f32[4,384,384]{1,2,0:T(8,128)S(1)}, f32[4,384,384]{1,2,0:T(8,128)}, u32[]{:S(2)}) copy-start(f32[4,384,384]{1,2,0:T(8,128)} %copy.25) | copy-start | bytes 7077892
  410.8 1.2 copy-start.4
  412.5 142.2 %copy-start.5 = (f32[4,256,256]{1,2,0:T(8,128)}, f32[4,256,256]{1,2,0:T(8,128)S(1)}, u32[]{:S(2)}) copy-start(f32[4,256,256]{1,2,0:T(8,128)S(1)} %fusion.249) | copy-start | bytes 3145732
  413.8 22.2 %collective-permute-start.8 = (f32[4,64,256]{1,2,0:T(8,128)}, f32[4,64,256]{1,2,0:T(8,128)S(1)}, u32[]{:S(2)}, u32[]{:S(2)}) collective-permute-start(f32[4,64,256]{1,2,0:T(8,128)} %get-tuple-element.754), channel_id=1, source_target_pairs={{0,8},{8,16},{16,24},{24,0},{1,9},{9,17},{17,25},{25,1},{2,10},{10... | collective-permute-start | bytes 786440 | tf_op jit(solution)/shard_map/ppermute | solution.py:22
  422.6 24.5 %collective-permute-start.9 = (f32[4,64,256]{1,2,0:T(8,128)}, f32[4,64,256]{1,2,0:T(8,128)}, u32[]{:S(2)}, u32[]{:S(2)}) collective-permute-start(f32[4,64,256]{1,2,0:T(8,128)} %get-tuple-element.755), channel_id=1, source_target_pairs={{8,0},{16,8},{24,16},{0,24},{9,1},{17,9},{25,17},{1,25},{10,2},{18... | collective-permute-start | bytes 786440 | tf_op jit(solution)/shard_map/ppermute | solution.py:25
  422.7 596.7 %all-reduce.13.cloned.1.call-start = ((), (), s32[]{:S(2)}) async-start(), calls=%async_computation.1 | async-start | bytes 1048576 | tf_op jit(solution)/shard_map/psum | solution.py:142
  436.0 17.0 %copy-start.11 = (f32[4,64,256]{1,2,0:T(8,128)}, f32[4,64,256]{1,2,0:T(8,128)S(1)}, u32[]{:S(2)}) copy-start(f32[4,64,256]{1,2,0:T(8,128)S(1)} %collective-permute-done.8) | copy-start | bytes 786436
  449.4 105.3 %collective-permute-start.10 = (f32[4,384,64]{1,2,0:T(8,128)}, f32[4,384,64]{1,2,0:T(8,128)S(1)}, u32[]{:S(2)}, u32[]{:S(2)}) collective-permute-start(f32[4,384,64]{1,2,0:T(8,128)} %get-tuple-element.750), channel_id=1, source_target_pairs={{0,1},{1,2},{2,3},{3,4},{4,5},{5,6},{6,7},{7,0},{8,9},{9,10},{10,1... | collective-permute-start | bytes 1179656 | tf_op jit(solution)/shard_map/ppermute | solution.py:22
  449.4 105.3 %collective-permute-start.11 = (f32[4,384,64]{1,2,0:T(8,128)}, f32[4,384,64]{1,2,0:T(8,128)}, u32[]{:S(2)}, u32[]{:S(2)}) collective-permute-start(f32[4,384,64]{1,2,0:T(8,128)} %get-tuple-element.751), channel_id=1, source_target_pairs={{1,0},{2,1},{3,2},{4,3},{5,4},{6,5},{7,6},{0,7},{9,8},{10,9},{11,1... | collective-permute-start | bytes 1179656 | tf_op jit(solution)/shard_map/ppermute | solution.py:25
  625.6 3.1 copy-start.7
  628.8 0.8 copy-start.8
  684.2 3.1 copy-start.7
  687.5 0.8 copy-start.8
  742.6 3.1 copy-start.7
  745.9 0.8 copy-start.8
  765.8 129.1 %collective-permute-start.12 = (f32[4,64,384]{2,1,0:T(8,128)S(1)}, f32[4,64,384]{2,1,0:T(8,128)S(1)}, u32[]{:S(2)}, u32[]{:S(2)}) collective-permute-start(f32[4,64,384]{2,1,0:T(8,128)S(1)} %get-tuple-element.746), channel_id=1, source_target_pairs={{0,8},{8,16},{16,24},{24,0},{1,9},{9,17},{17,25},{25,1},{2,10},{10... | collective-permute-start | bytes 1179656 | tf_op jit(solution)/shard_map/ppermute | solution.py:22
  765.8 129.3 %collective-permute-start.13 = (f32[4,64,384]{2,1,0:T(8,128)S(1)}, f32[4,64,384]{2,1,0:T(8,128)S(1)}, u32[]{:S(2)}, u32[]{:S(2)}) collective-permute-start(f32[4,64,384]{2,1,0:T(8,128)S(1)} %get-tuple-element.747), channel_id=1, source_target_pairs={{8,0},{16,8},{24,16},{0,24},{9,1},{17,9},{25,17},{1,25},{10,2},{18... | collective-permute-start | bytes 1179656 | tf_op jit(solution)/shard_map/ppermute | solution.py:25
  898.0 123.3 %collective-permute-start.14 = (f32[4,512,64]{1,2,0:T(8,128)}, f32[4,512,64]{1,2,0:T(8,128)S(1)}, u32[]{:S(2)}, u32[]{:S(2)}) collective-permute-start(f32[4,512,64]{1,2,0:T(8,128)} %get-tuple-element.738), channel_id=1, source_target_pairs={{0,1},{1,2},{2,3},{3,4},{4,5},{5,6},{6,7},{7,0},{8,9},{9,10},{10,1... | collective-permute-start | bytes 1572872 | tf_op jit(solution)/shard_map/ppermute | solution.py:22
  898.1 123.1 %collective-permute-start.15 = (f32[4,512,64]{1,2,0:T(8,128)}, f32[4,512,64]{1,2,0:T(8,128)S(1)}, u32[]{:S(2)}, u32[]{:S(2)}) collective-permute-start(f32[4,512,64]{1,2,0:T(8,128)} %get-tuple-element.739), channel_id=1, source_target_pairs={{1,0},{2,1},{3,2},{4,3},{5,4},{6,5},{7,6},{0,7},{9,8},{10,9},{11,1... | collective-permute-start | bytes 1572872 | tf_op jit(solution)/shard_map/ppermute | solution.py:25
  1021.2 3.0 copy-start.1
  1025.8 1.2 copy-start.6
Sparse Core Ops, SparseCore 0:
  422.8 130.7 all-reduce.10
  888.2 131.0 all-reduce.12
where the time goes:
time: 1050 us; the launch traced here: 1040 us
  waiting for transfers between devices  289 us (28%)
  starting transfers between devices  264 us (25%)
  matrix products  211 us (20%)
  local copies, waits for them, and re-layouts  128 us (12%)
  loops' own time  85.2 us (8%)
  other arithmetic  42.3 us (4%)
  between operations  15.9 us (2%)
    ppermute x8, starting transfers between devices, extended_2(): lax.ppermute(lax.slice_in_dim(block, 0, width, axis=dim), axis, backward)  248 us
    psum x2, waiting for transfers between devices, body(): summed = lax.psum(probe_grad, ('ty', 'tx'))  217 us
    dot_general x196, matrix products, matmul(): jnp.dot(left, right, precision=lax.Precision.HIGHEST, preferred_element_t...  211 us
    another operation x2, loops' own time, body(): grads, probe_grad = lax.fori_loop(zero, count, visit, start)  85.2 us
    dynamic_update_slice x6, local copies, waits for them, and re-layouts, visit(): lax.dynamic_update_slice(local, current + object_part, (zero, top, left))  68.5 us
    ppermute x8, waiting for transfers between devices, extended_2(): lax.ppermute(lax.slice_in_dim(block, block.shape[dim] - width, None, axis...  46.6 us
    ppermute x8, waiting for transfers between devices, extended_2(): lax.ppermute(lax.slice_in_dim(block, 0, width, axis=dim), axis, backward)  25.5 us
  transfers between devices with their start and end apart: 18, of which 12 were waited for; matrix products, arithmetic and copies ran while one was open for 2% of the time, Pallas kernels for 0%

commit v1 on v0

--- a/solution.py
+++ b/solution.py
@@ -139,7 +139,7 @@
         core = core - object_rate / peak * total
         if step + 1 < ITERS:
             extended = extended_2(core, (("ty", 1), ("tx", 2)), MARGIN)
-        summed = lax.psum(probe_grad, ("ty", "tx"))
+        summed = lax.psum(lax.psum(probe_grad, axis_name="tx"), axis_name="ty")
         probe_now = probe_now - probe_rate / devices * summed
     return (core.reshape(2, 2, CORE, CORE), probe_now)
 

time: 1050 us -> 975 us (0.929)
  waiting for transfers between devices: 289 us -> 223 us
    psum x2 -> x4, waiting for transfers between devices: 217 us -> 167 us  [body(): summed = lax.psum(lax.psum(probe_grad, axis_name='tx'), axis_name='ty')]
    ppermute x8, waiting for transfers between devices: 46.6 us -> 33.5 us  [extended_2(): lax.ppermute(lax.slice_in_dim(block, block.shape[dim] - width, None, axis...]
  transfers between devices with their start and end apart: 18 -> 20, of which waited for: 12 -> 11; matrix products, arithmetic and copies ran while one was open for 2% -> 3% of each run, Pallas kernels for 0% -> 0%
where the time goes in v1:
time: 975 us; the launch traced here: 963 us
  starting transfers between devices  258 us (26%)
  waiting for transfers between devices  223 us (23%)
  matrix products  211 us (22%)
  local copies, waits for them, and re-layouts  128 us (13%)
  loops' own time  86.4 us (9%)
  other arithmetic  41.5 us (4%)
  between operations  15.6 us (2%)
    ppermute x8, starting transfers between devices, extended_2(): lax.ppermute(lax.slice_in_dim(block, 0, width, axis=dim), axis, backward)  249 us
    dot_general x196, matrix products, matmul(): jnp.dot(left, right, precision=lax.Precision.HIGHEST, preferred_element_t...  211 us
    psum x4, waiting for transfers between devices, body(): summed = lax.psum(lax.psum(probe_grad, axis_name='tx'), axis_name='ty')  167 us
    another operation x2, loops' own time, body(): grads, probe_grad = lax.fori_loop(zero, count, visit, start)  86.4 us
    dynamic_update_slice x6, local copies, waits for them, and re-layouts, visit(): lax.dynamic_update_slice(local, current + object_part, (zero, top, left))  68.5 us
    ppermute x8, waiting for transfers between devices, extended_2(): lax.ppermute(lax.slice_in_dim(block, block.shape[dim] - width, None, axis...  33.5 us
    ppermute x8, waiting for transfers between devices, extended_2(): lax.ppermute(lax.slice_in_dim(block, 0, width, axis=dim), axis, backward)  21.9 us
  transfers between devices with their start and end apart: 20, of which 11 were waited for; matrix products, arithmetic and copies ran while one was open for 3% of the time, Pallas kernels for 0%

profile of v1, /device:TPU:0, one launch (start us, length us, event | category | flops | bytes accessed | tf_op | source)
XLA Modules:
  0.0 962.9 jit_solution(12940458433252814597)
XLA Ops:
  7.2 1.6 copy.21
  10.1 3.0 collective-permute-start
  17.2 9.8 %collective-permute-done = f32[4,64,256]{1,2,0:T(8,128)S(1)} collective-permute-done((f32[4,64,256]{1,2,0:T(8,128)}, f32[4,64,256]{1,2,0:T(8,128)S(1)}, u32[]{:S(2)}, u32[]{:S(2)}) %collective-permute-start) | collective-permute-done | bytes 262176 | tf_op jit(solution)/shard_map/ppermute | solution.py:22
  27.0 10.6 %collective-permute-done.1 = f32[4,64,256]{1,2,0:T(8,128)S(1)} collective-permute-done((f32[4,64,256]{1,2,0:T(8,128)}, f32[4,64,256]{1,2,0:T(8,128)S(1)}, u32[]{:S(2)}, u32[]{:S(2)}) %collective-permute-start.1) | collective-permute-done | bytes 262176 | tf_op jit(solution)/shard_map/ppermute | solution.py:25
  38.0 3.5 collective-permute-start.3
  44.5 4.6 collective-permute-done.2
  49.1 3.1 pad_maximum_fusion.2
  52.2 1.6 broadcast.114.clone
  54.7 204.0 %while.32 = (s32[]{:T(128)}, f32[4,384,384]{2,1,0:T(8,128)}, f32[2,256,256]{2,1,0:T(8,128)}, s32[]{:T(128)}, s32[1,1,5,2]{2,3,1,0:T(2,128)S(1)}, /*index=5*/f32[...) while((s32[]{:T(128)}, f32[4,384,384]{2,1,0:T(8,128)}, ...), condition=%wide.region_2.3_spmd.clone.clone, body=%wide.region_1.2_spmd.clone.clone.sunk | while | flops 6464077824 | bytes 48234916 | solution.py:135
  83.6 2.5 fusion.635
  103.9 2.4 fusion.646
  116.6 1.6 fusion.651
  123.3 2.0 maximum_add_fusion.8
  125.3 11.5 %dynamic_update_slice.16 = f32[4,384,384]{2,1,0:T(8,128)} dynamic-update-slice(f32[4,384,384]{2,1,0:T(8,128)} %get-tuple-element.1014, f32[4,256,256]{2,1,0:T(8,128)S(1)} %maximum_add_fusion.8, s32[]{:T(128)} %constant.70.clone.1..sunk, s32[]{:T(128)S(6)} %select_n.366, s32[]{:T(128)S(6)} %select_n.367) | dynamic-update-slice | bytes 2097156 | tf_op jit(solution)/shard_map/while/body/dynamic_update_slice | solution.py:128
  141.8 2.5 fusion.635
  162.1 2.4 fusion.646
  174.9 1.6 fusion.651
  181.5 2.0 maximum_add_fusion.8
  183.5 11.2 %dynamic_update_slice.16 = f32[4,384,384]{2,1,0:T(8,128)} dynamic-update-slice(f32[4,384,384]{2,1,0:T(8,128)} %get-tuple-element.1014, f32[4,256,256]{2,1,0:T(8,128)S(1)} %maximum_add_fusion.8, s32[]{:T(128)} %constant.70.clone.1..sunk, s32[]{:T(128)S(6)} %select_n.366, s32[]{:T(128)S(6)} %select_n.367) | dynamic-update-slice | bytes 2097156 | tf_op jit(solution)/shard_map/while/body/dynamic_update_slice | solution.py:128
  199.8 2.5 fusion.635
  220.0 2.4 fusion.646
  232.8 1.6 fusion.651
  239.5 2.0 maximum_add_fusion.8
  241.5 11.5 %dynamic_update_slice.16 = f32[4,384,384]{2,1,0:T(8,128)} dynamic-update-slice(f32[4,384,384]{2,1,0:T(8,128)} %get-tuple-element.1014, f32[4,256,256]{2,1,0:T(8,128)S(1)} %maximum_add_fusion.8, s32[]{:T(128)} %constant.70.clone.1..sunk, s32[]{:T(128)S(6)} %select_n.366, s32[]{:T(128)S(6)} %select_n.367) | dynamic-update-slice | bytes 2097156 | tf_op jit(solution)/shard_map/while/body/dynamic_update_slice | solution.py:128
  259.9 117.3 %collective-permute-start.5 = (f32[4,64,384]{2,1,0:T(8,128)S(1)}, f32[4,64,384]{2,1,0:T(8,128)S(1)}, u32[]{:S(2)}, u32[]{:S(2)}) collective-permute-start(f32[4,64,384]{2,1,0:T(8,128)S(1)} %get-tuple-element.749), channel_id=1, source_target_pairs={{8,0},{16,8},{24,16},{0,24},{9,1},{17,9},{25,17},{1,25},{10,2},{18... | collective-permute-start | bytes 1179656 | tf_op jit(solution)/shard_map/ppermute | solution.py:25
  377.2 3.1 copy.25
  380.3 4.3 collective-permute-done.4
  387.0 2.5 pad_maximum_fusion.9
  389.5 4.3 collective-permute-start.6
  395.2 63.5 %all-reduce.13.cloned.1.call-done = f32[2,256,256]{2,1,0:T(8,128)} async-done(((f32[2,256,256]{2,1,0:T(8,128)}), f32[2,256,256]{2,1,0:T(8,128)}) %all-reduce.13.cloned.1.call-update) | async-done | bytes 524304 | tf_op jit(solution)/shard_map/psum | solution.py:142
  458.8 3.2 pad_maximum_fusion
  462.0 2.8 fusion.242
  466.8 1.5 collective-permute-start.8
  469.8 14.8 %collective-permute-done.8 = f32[4,64,256]{1,2,0:T(8,128)S(1)} collective-permute-done((f32[4,64,256]{1,2,0:T(8,128)S(1)}, f32[4,64,256]{1,2,0:T(8,128)S(1)}, u32[]{:S(2)}, u32[]{:S(2)}) %collective-permute-start.8) | collective-permute-done | bytes 262176 | tf_op jit(solution)/shard_map/ppermute | solution.py:22
  484.6 10.3 %collective-permute-done.9 = f32[4,64,256]{1,2,0:T(8,128)S(1)} collective-permute-done((f32[4,64,256]{1,2,0:T(8,128)S(1)}, f32[4,64,256]{1,2,0:T(8,128)S(1)}, u32[]{:S(2)}, u32[]{:S(2)}) %collective-permute-start.9) | collective-permute-done | bytes 262176 | tf_op jit(solution)/shard_map/ppermute | solution.py:25
  496.9 3.5 collective-permute-start.11
  500.4 10.1 %all-reduce.15.cloned.1.call-done = f32[2,256,256]{2,1,0:T(8,128)} async-done(((f32[2,256,256]{2,1,0:T(8,128)}), f32[2,256,256]{2,1,0:T(8,128)}) %all-reduce.15.cloned.1.call-update) | async-done | bytes 524304 | tf_op jit(solution)/shard_map/psum | solution.py:142
  511.6 3.4 pad_maximum_fusion.3
  515.0 1.6 broadcast.114
  517.4 204.6 %while.33 = (s32[]{:T(128)}, f32[4,384,384]{2,1,0:T(8,128)}, f32[2,256,256]{2,1,0:T(8,128)}, s32[]{:T(128)}, s32[1,1,5,2]{2,3,1,0:T(2,128)S(1)}, /*index=5*/f32[...) while((s32[]{:T(128)}, f32[4,384,384]{2,1,0:T(8,128)}, ...), condition=%wide.region_7.8_spmd.clone.clone, body=%wide.region_6.7_spmd.clone.clone.sunk | while | flops 6464077824 | bytes 48234916 | solution.py:135
  546.3 2.5 fusion.709
  566.5 2.4 fusion.720
  579.3 1.6 fusion.725
  586.7 1.8 maximum_add_fusion.10
  588.5 11.5 %dynamic_update_slice.17 = f32[4,384,384]{2,1,0:T(8,128)} dynamic-update-slice(f32[4,384,384]{2,1,0:T(8,128)} %get-tuple-element.1071, f32[4,256,256]{2,1,0:T(8,128)S(1)} %maximum_add_fusion.10, s32[]{:T(128)} %constant.70.clone.1..sunk.1, s32[]{:T(128)S(6)} %select_n.385, s32[]{:T(128)S(6)} %select_n.386) | dynamic-update-slice | bytes 2097156 | tf_op jit(solution)/shard_map/while/body/dynamic_update_slice | solution.py:128
  605.1 2.5 fusion.709
  625.3 2.4 fusion.720
  638.1 1.6 fusion.725
  645.5 1.8 maximum_add_fusion.10
  647.3 11.2 %dynamic_update_slice.17 = f32[4,384,384]{2,1,0:T(8,128)} dynamic-update-slice(f32[4,384,384]{2,1,0:T(8,128)} %get-tuple-element.1071, f32[4,256,256]{2,1,0:T(8,128)S(1)} %maximum_add_fusion.10, s32[]{:T(128)} %constant.70.clone.1..sunk.1, s32[]{:T(128)S(6)} %select_n.385, s32[]{:T(128)S(6)} %select_n.386) | dynamic-update-slice | bytes 2097156 | tf_op jit(solution)/shard_map/while/body/dynamic_update_slice | solution.py:128
  663.6 2.5 fusion.709
  683.9 2.4 fusion.720
  696.6 1.6 fusion.725
  704.1 1.8 maximum_add_fusion.10
  705.9 11.5 %dynamic_update_slice.17 = f32[4,384,384]{2,1,0:T(8,128)} dynamic-update-slice(f32[4,384,384]{2,1,0:T(8,128)} %get-tuple-element.1071, f32[4,256,256]{2,1,0:T(8,128)S(1)} %maximum_add_fusion.10, s32[]{:T(128)} %constant.70.clone.1..sunk.1, s32[]{:T(128)S(6)} %select_n.385, s32[]{:T(128)S(6)} %select_n.386) | dynamic-update-slice | bytes 2097156 | tf_op jit(solution)/shard_map/while/body/dynamic_update_slice | solution.py:128
  723.3 118.5 %collective-permute-start.13 = (f32[4,64,384]{2,1,0:T(8,128)S(1)}, f32[4,64,384]{2,1,0:T(8,128)S(1)}, u32[]{:S(2)}, u32[]{:S(2)}) collective-permute-start(f32[4,64,384]{2,1,0:T(8,128)S(1)} %get-tuple-element.747), channel_id=1, source_target_pairs={{8,0},{16,8},{24,16},{0,24},{9,1},{17,9},{25,17},{1,25},{10,2},{18... | collective-permute-start | bytes 1179656 | tf_op jit(solution)/shard_map/ppermute | solution.py:25
  841.9 57.4 %all-reduce.17.cloned.1.call-done = f32[2,256,256]{2,1,0:T(8,128)} async-done(((f32[2,256,256]{2,1,0:T(8,128)}), f32[2,256,256]{2,1,0:T(8,128)}) %all-reduce.17.cloned.1.call-update) | async-done | bytes 524304 | tf_op jit(solution)/shard_map/psum | solution.py:142
  899.3 3.1 copy.30
  902.9 2.5 pad_maximum_fusion.6
  905.4 3.5 collective-permute-start.15
  910.3 36.3 %all-reduce.19.cloned.1.call-done = f32[2,256,256]{2,1,0:T(8,128)} async-done(((f32[2,256,256]{2,1,0:T(8,128)}), f32[2,256,256]{2,1,0:T(8,128)}) %all-reduce.19.cloned.1.call-update) | async-done | bytes 524304 | tf_op jit(solution)/shard_map/psum | solution.py:142
  946.6 1.9 multiply_subtract_fusion
  948.5 2.9 pad_maximum_fusion.1
  951.5 1.6 fusion.240
  (323 shorter events, 230.2 us)
Async XLA Ops:
  7.2 451.6 %all-reduce.13.cloned.1.call-start = ((), (), s32[]{:S(2)}) async-start(), calls=%async_computation | async-start | bytes 1048576 | tf_op jit(solution)/shard_map/psum | solution.py:142
  8.8 40.4 %copy-start.3 = (f32[2,2,256,256]{2,3,1,0:T(8,128)}, f32[2,2,256,256]{2,3,1,0:T(8,128)S(1)}, u32[]{:S(2)}) copy-start(f32[2,2,256,256]{2,3,1,0:T(8,128)S(1)} %copy.21) | copy-start | bytes 3145732
  10.1 16.9 %collective-permute-start = (f32[4,64,256]{1,2,0:T(8,128)}, f32[4,64,256]{1,2,0:T(8,128)S(1)}, u32[]{:S(2)}, u32[]{:S(2)}) collective-permute-start(f32[4,64,256]{1,2,0:T(8,128)} %get-tuple-element.756), channel_id=1, source_target_pairs={{0,8},{8,16},{16,24},{24,0},{1,9},{9,17},{17,25},{25,1},{2,10},{10... | collective-permute-start | bytes 786440 | tf_op jit(solution)/shard_map/ppermute | solution.py:22
  13.1 24.6 %collective-permute-start.1 = (f32[4,64,256]{1,2,0:T(8,128)}, f32[4,64,256]{1,2,0:T(8,128)S(1)}, u32[]{:S(2)}, u32[]{:S(2)}) collective-permute-start(f32[4,64,256]{1,2,0:T(8,128)} %get-tuple-element.757), channel_id=1, source_target_pairs={{8,0},{16,8},{24,16},{0,24},{9,1},{17,9},{25,17},{1,25},{10,2},{18... | collective-permute-start | bytes 786440 | tf_op jit(solution)/shard_map/ppermute | solution.py:25
  37.6 5.4 copy-start.11
  38.0 11.2 %collective-permute-start.2 = (f32[4,384,64]{1,2,0:T(8,128)S(1)}, f32[4,384,64]{1,2,0:T(8,128)S(1)}, u32[]{:S(2)}, u32[]{:S(2)}) collective-permute-start(f32[4,384,64]{1,2,0:T(8,128)S(1)} %get-tuple-element.752), channel_id=1, source_target_pairs={{0,1},{1,2},{2,3},{3,4},{4,5},{5,6},{6,7},{7,0},{8,9},{9,10},{10,1... | collective-permute-start | bytes 1179656 | tf_op jit(solution)/shard_map/ppermute | solution.py:22
  38.0 11.1 %collective-permute-start.3 = (f32[4,384,64]{1,2,0:T(8,128)S(1)}, f32[4,384,64]{1,2,0:T(8,128)S(1)}, u32[]{:S(2)}, u32[]{:S(2)}) collective-permute-start(f32[4,384,64]{1,2,0:T(8,128)S(1)} %get-tuple-element.753), channel_id=1, source_target_pairs={{1,0},{2,1},{3,2},{4,3},{5,4},{6,5},{7,6},{0,7},{9,8},{10,9},{11,1... | collective-permute-start | bytes 1179656 | tf_op jit(solution)/shard_map/ppermute | solution.py:25
  44.5 10.1 %copy-start = (f32[2,256,256]{2,1,0:T(8,128)S(1)}, f32[2,256,256]{2,1,0:T(8,128)}, u32[]{:S(2)}) copy-start(f32[2,256,256]{2,1,0:T(8,128)} %param.10) | copy-start | bytes 1572868
  44.5 10.1 %copy-start.14 = (s32[1,1,5,2]{2,3,1,0:T(2,128)S(1)}, s32[1,1,5,2]{2,3,1,0:T(2,128)}, u32[]{:S(2)}) copy-start(s32[1,1,5,2]{2,3,1,0:T(2,128)} %param.12) | copy-start | bytes 124
  120.0 3.1 copy-start.9
  123.3 13.5 %copy-start.10 = (f32[2,256,256]{2,1,0:T(8,128)}, f32[2,256,256]{2,1,0:T(8,128)S(1)}, u32[]{:S(2)}) copy-start(f32[2,256,256]{2,1,0:T(8,128)S(1)} %maximum_add_fusion.9) | copy-start | bytes 1572868 | tf_op jit(solution)/shard_map/while
  178.2 3.1 copy-start.9
  181.5 13.2 %copy-start.10 = (f32[2,256,256]{2,1,0:T(8,128)}, f32[2,256,256]{2,1,0:T(8,128)S(1)}, u32[]{:S(2)}) copy-start(f32[2,256,256]{2,1,0:T(8,128)S(1)} %maximum_add_fusion.9) | copy-start | bytes 1572868 | tf_op jit(solution)/shard_map/while
  236.2 3.1 copy-start.9
  239.5 13.5 %copy-start.10 = (f32[2,256,256]{2,1,0:T(8,128)}, f32[2,256,256]{2,1,0:T(8,128)S(1)}, u32[]{:S(2)}) copy-start(f32[2,256,256]{2,1,0:T(8,128)S(1)} %maximum_add_fusion.9) | copy-start | bytes 1572868 | tf_op jit(solution)/shard_map/while
  259.9 124.7 %collective-permute-start.4 = (f32[4,64,384]{2,1,0:T(8,128)S(1)}, f32[4,64,384]{2,1,0:T(8,128)}, u32[]{:S(2)}, u32[]{:S(2)}) collective-permute-start(f32[4,64,384]{2,1,0:T(8,128)S(1)} %get-tuple-element.748), channel_id=1, source_target_pairs={{0,8},{8,16},{16,24},{24,0},{1,9},{9,17},{17,25},{25,1},{2,10},{10... | collective-permute-start | bytes 1179656 | tf_op jit(solution)/shard_map/ppermute | solution.py:22
  259.9 126.8 %collective-permute-start.5 = (f32[4,64,384]{2,1,0:T(8,128)S(1)}, f32[4,64,384]{2,1,0:T(8,128)S(1)}, u32[]{:S(2)}, u32[]{:S(2)}) collective-permute-start(f32[4,64,384]{2,1,0:T(8,128)S(1)} %get-tuple-element.749), channel_id=1, source_target_pairs={{8,0},{16,8},{24,16},{0,24},{9,1},{17,9},{25,17},{1,25},{10,2},{18... | collective-permute-start | bytes 1179656 | tf_op jit(solution)/shard_map/ppermute | solution.py:25
  389.5 69.3 %collective-permute-start.6 = (f32[4,512,64]{1,2,0:T(8,128)}, f32[4,512,64]{1,2,0:T(8,128)}, u32[]{:S(2)}, u32[]{:S(2)}) collective-permute-start(f32[4,512,64]{1,2,0:T(8,128)} %get-tuple-element.740), channel_id=1, source_target_pairs={{0,1},{1,2},{2,3},{3,4},{4,5},{5,6},{6,7},{7,0},{8,9},{9,10},{10,1... | collective-permute-start | bytes 1572872 | tf_op jit(solution)/shard_map/ppermute | solution.py:22
  393.8 65.0 %collective-permute-start.7 = (f32[4,512,64]{1,2,0:T(8,128)}, f32[4,512,64]{1,2,0:T(8,128)}, u32[]{:S(2)}, u32[]{:S(2)}) collective-permute-start(f32[4,512,64]{1,2,0:T(8,128)} %get-tuple-element.741), channel_id=1, source_target_pairs={{1,0},{2,1},{3,2},{4,3},{5,4},{6,5},{7,6},{0,7},{9,8},{10,9},{11,1... | collective-permute-start | bytes 1572872 | tf_op jit(solution)/shard_map/ppermute | solution.py:25
  393.9 116.6 %all-reduce.15.cloned.1.call-start = ((), (), s32[]{:S(2)}) async-start(), calls=%async_computation.1 | async-start | bytes 1048576 | tf_op jit(solution)/shard_map/psum | solution.py:142
  458.8 440.5 %all-reduce.17.cloned.1.call-start = ((), (), s32[]{:S(2)}) async-start(), calls=%async_computation.2 | async-start | bytes 1048576 | tf_op jit(solution)/shard_map/psum | solution.py:142
  458.8 3.2 copy-start.1
  464.9 1.2 copy-start.4
  466.6 45.0 %copy-start.5 = (f32[4,256,256]{1,2,0:T(8,128)}, f32[4,256,256]{1,2,0:T(8,128)S(1)}, u32[]{:S(2)}) copy-start(f32[4,256,256]{1,2,0:T(8,128)S(1)} %fusion.249) | copy-start | bytes 3145732
  466.8 17.8 %collective-permute-start.8 = (f32[4,64,256]{1,2,0:T(8,128)S(1)}, f32[4,64,256]{1,2,0:T(8,128)S(1)}, u32[]{:S(2)}, u32[]{:S(2)}) collective-permute-start(f32[4,64,256]{1,2,0:T(8,128)S(1)} %get-tuple-element.754), channel_id=1, source_target_pairs={{0,8},{8,16},{16,24},{24,0},{1,9},{9,17},{17,25},{25,1},{2,10},{10... | collective-permute-start | bytes 786440 | tf_op jit(solution)/shard_map/ppermute | solution.py:22
  468.3 26.5 %collective-permute-start.9 = (f32[4,64,256]{1,2,0:T(8,128)S(1)}, f32[4,64,256]{1,2,0:T(8,128)S(1)}, u32[]{:S(2)}, u32[]{:S(2)}) collective-permute-start(f32[4,64,256]{1,2,0:T(8,128)S(1)} %get-tuple-element.755), channel_id=1, source_target_pairs={{8,0},{16,8},{24,16},{0,24},{9,1},{17,9},{25,17},{1,25},{10,2},{18... | collective-permute-start | bytes 786440 | tf_op jit(solution)/shard_map/ppermute | solution.py:25
  484.6 15.9 %copy-start.12 = (f32[4,64,256]{1,2,0:T(8,128)}, f32[4,64,256]{1,2,0:T(8,128)S(1)}, u32[]{:S(2)}) copy-start(f32[4,64,256]{1,2,0:T(8,128)S(1)} %collective-permute-done.8) | copy-start | bytes 786436
  494.8 0.8 copy-start.13
  496.9 14.7 %collective-permute-start.10 = (f32[4,384,64]{1,2,0:T(8,128)}, f32[4,384,64]{1,2,0:T(8,128)S(1)}, u32[]{:S(2)}, u32[]{:S(2)}) collective-permute-start(f32[4,384,64]{1,2,0:T(8,128)} %get-tuple-element.750), channel_id=1, source_target_pairs={{0,1},{1,2},{2,3},{3,4},{4,5},{5,6},{6,7},{7,0},{8,9},{9,10},{10,1... | collective-permute-start | bytes 1179656 | tf_op jit(solution)/shard_map/ppermute | solution.py:22
  496.9 14.7 %collective-permute-start.11 = (f32[4,384,64]{1,2,0:T(8,128)}, f32[4,384,64]{1,2,0:T(8,128)}, u32[]{:S(2)}, u32[]{:S(2)}) collective-permute-start(f32[4,384,64]{1,2,0:T(8,128)} %get-tuple-element.751), channel_id=1, source_target_pairs={{1,0},{2,1},{3,2},{4,3},{5,4},{6,5},{7,6},{0,7},{9,8},{10,9},{11,1... | collective-permute-start | bytes 1179656 | tf_op jit(solution)/shard_map/ppermute | solution.py:25
  582.7 3.1 copy-start.7
  585.9 0.8 copy-start.8
  641.5 3.1 copy-start.7
  644.7 0.8 copy-start.8
  700.0 3.1 copy-start.7
  703.3 0.8 copy-start.8
  723.3 179.1 %collective-permute-start.12 = (f32[4,64,384]{2,1,0:T(8,128)S(1)}, f32[4,64,384]{2,1,0:T(8,128)S(1)}, u32[]{:S(2)}, u32[]{:S(2)}) collective-permute-start(f32[4,64,384]{2,1,0:T(8,128)S(1)} %get-tuple-element.746), channel_id=1, source_target_pairs={{0,8},{8,16},{16,24},{24,0},{1,9},{9,17},{17,25},{25,1},{2,10},{10... | collective-permute-start | bytes 1179656 | tf_op jit(solution)/shard_map/ppermute | solution.py:22
  723.3 179.3 %collective-permute-start.13 = (f32[4,64,384]{2,1,0:T(8,128)S(1)}, f32[4,64,384]{2,1,0:T(8,128)S(1)}, u32[]{:S(2)}, u32[]{:S(2)}) collective-permute-start(f32[4,64,384]{2,1,0:T(8,128)S(1)} %get-tuple-element.747), channel_id=1, source_target_pairs={{8,0},{16,8},{24,16},{0,24},{9,1},{17,9},{25,17},{1,25},{10,2},{18... | collective-permute-start | bytes 1179656 | tf_op jit(solution)/shard_map/ppermute | solution.py:25
  841.8 104.8 %all-reduce.19.cloned.1.call-start = ((), (), s32[]{:S(2)}) async-start(), calls=%async_computation.3 | async-start | bytes 1048576 | tf_op jit(solution)/shard_map/psum | solution.py:142
  905.4 43.1 %collective-permute-start.14 = (f32[4,512,64]{1,2,0:T(8,128)}, f32[4,512,64]{1,2,0:T(8,128)S(1)}, u32[]{:S(2)}, u32[]{:S(2)}) collective-permute-start(f32[4,512,64]{1,2,0:T(8,128)} %get-tuple-element.738), channel_id=1, source_target_pairs={{0,1},{1,2},{2,3},{3,4},{4,5},{5,6},{6,7},{7,0},{8,9},{9,10},{10,1... | collective-permute-start | bytes 1572872 | tf_op jit(solution)/shard_map/ppermute | solution.py:22
  905.4 43.1 %collective-permute-start.15 = (f32[4,512,64]{1,2,0:T(8,128)}, f32[4,512,64]{1,2,0:T(8,128)S(1)}, u32[]{:S(2)}, u32[]{:S(2)}) collective-permute-start(f32[4,512,64]{1,2,0:T(8,128)} %get-tuple-element.739), channel_id=1, source_target_pairs={{1,0},{2,1},{3,2},{4,3},{5,4},{6,5},{7,6},{0,7},{9,8},{10,9},{11,1... | collective-permute-start | bytes 1572872 | tf_op jit(solution)/shard_map/ppermute | solution.py:25
  948.5 3.0 copy-start.2
  953.1 1.2 copy-start.6
Sparse Core Ops, SparseCore 0:
  394.1 64.6 all-reduce.12
  461.7 48.7 all-reduce.14
  841.9 57.2 all-reduce.16
  902.1 44.4 all-reduce.18
